TPU v7x, 1024 devices: a whole 8x8x8 slice. The times are simulated.
1024 devices in a mesh: curve: 64 (over y, x), lev: 16 (over z, core).
Axes of the slice: x: 8, y: 8, z: 8, core: 2. Of those that a mesh axis runs over, the one named last changes fastest.
Arguments:
- source_field: bfloat16 [1048576, 1024], P(('curve', 'lev')), may hold values from -6 to 6
- slot_elems: int32 [16, 131072], P(None, ('curve', 'lev')), may hold values from 0 to 1023
- slot_tiles: int32 [131072], P(('curve', 'lev')), may hold values from 0 to 16383, as said below
- weights: bfloat16 [131072, 16, 256], P(('curve', 'lev')), may hold values from -0.375 to 0.375
Outputs:
- remapped: float32 [64, 262144], P(None, ('curve', 'lev'))
Inputs may be any that keep to these rules, and one draw needn't show every extreme that they name: `slot_elems`: local element ids within the slot's own device's elements. `slot_tiles`: tile g belongs to band g // 256. The 128 slots of a device with curve index b name tiles of the 4 bands b to b + 4 - 1 modulo 64 only, at most 64 of them in one band, a bound reached on every device, and exactly 2 tiles of each residue modulo 64.
All inputs are finite; a program needn't handle non-finite values.
Results may differ from a plain program's by a relative error of at most 0.0003.
Values sent between devices are 32-bit elements; how exact they have to be, the bound alone decides.
No kernel may reach another device: no remote copies, remote signals or barrier semaphores. Data moves between devices by JAX's collectives and lax.ppermute only.
A program may use at most 64 MiB of HBM per device.

v0:
```python
import jax
import jax.numpy as jnp
from jax import lax
from jax.sharding import PartitionSpec as P

NB = 4
CELL_DEV = 256


def shifted(block, axis, distance):
    devices = range(lax.axis_size(axis))
    route = [((i - distance) % len(devices), i) for i in devices]
    return lax.ppermute(block, axis, route)


def split_up(x, dim, size):
    before, after = (x.shape[:dim], x.shape[dim + 1 :])
    return jnp.moveaxis(x.reshape(*before, size, -1, *after), dim, 0)


def summed_on_arrival(x, axis, dim):
    pieces = split_up(x, dim, lax.axis_size(axis))
    arrived = lax.all_to_all(pieces, axis, split_axis=0, concat_axis=0, tiled=True)
    return arrived.sum(axis=0)


def deposit(band_total, received, arrived, band_tiles):
    tile_ids = arrived.astype(jnp.int32)
    dest_row = jnp.where(tile_ids >= 0, tile_ids % band_tiles, band_tiles)
    return band_total.at[dest_row].add(received, mode="drop")


def per_device(source_field, slot_elems, slot_tiles, weights):
    curve_size = lax.axis_size("curve")
    lev_size = lax.axis_size("lev")
    slot_count = slot_tiles.shape[0]
    tile_cells = weights.shape[1]
    node_cols = weights.shape[2]
    channels = source_field.shape[1] * slot_elems.shape[0] // node_cols
    row_width = channels * tile_cells
    band_tiles = CELL_DEV * lev_size // tile_cells
    gathered = jnp.take(source_field, jnp.transpose(slot_elems), axis=0)
    values = gathered.reshape(slot_count, node_cols, channels)
    partial_value = jnp.einsum("jnc,jtn->jct", values, weights, preferred_element_type=jnp.float32)
    partial_value = partial_value.reshape(slot_count, row_width)
    tile_tags = slot_tiles.astype(jnp.float32)
    band_index = lax.axis_index("curve")
    capacity = slot_count // 2
    slot_band = slot_tiles // band_tiles
    band_total = jnp.zeros((band_tiles, row_width), jnp.float32)
    for offset in range(NB):
        target = (band_index + offset) % curve_size
        chosen = slot_band == target
        slot_rank = jnp.cumsum(chosen.astype(jnp.int32)) - 1
        position = jnp.where(chosen, slot_rank, capacity)
        sending = (
            jnp.zeros((capacity, row_width), jnp.float32)
            .at[position]
            .set(partial_value, mode="drop")
        )
        sent_tags = (
            jnp.full((capacity,), -1.0, jnp.float32).at[position].set(tile_tags, mode="drop")
        )
        received, arrived = shifted((sending, sent_tags), "curve", offset)
        band_total = deposit(band_total, received, arrived, band_tiles)
    box_sums = summed_on_arrival(band_total, "lev", 0)
    return jnp.transpose(box_sums.reshape(-1, channels, tile_cells), (1, 0, 2)).reshape(
        channels, -1
    )


def solution(mesh):
    placed = (
        P(("curve", "lev"), None),
        P(None, ("curve", "lev")),
        P(("curve", "lev")),
        P(("curve", "lev"), None, None),
    )
    return jax.shard_map(
        per_device, mesh=mesh, in_specs=placed, out_specs=P(None, ("curve", "lev")), check_vma=False
    )
```

profile of v0, /device:TPU:1, one launch (start us, length us, event | category | flops | bytes accessed | tf_op | source)
XLA Modules:
  0.0 143.0 jit_solution(16059206408475999464)
XLA Ops:
  0.0 0.0 copy-start
  0.0 0.8 compare_select_fusion
  0.9 0.7 compare_and_fusion
  1.6 0.7 fusion.17
  2.2 0.1 copy.35
  2.3 0.2 reduce-window.36
  2.5 0.1 copy.41
  2.6 0.2 reduce-window.37
  2.8 0.1 copy.43
  2.9 0.2 reduce-window.38
  3.1 0.1 copy.45
  3.2 0.2 reduce-window.39
  3.4 0.1 copy.37
  3.5 0.1 reshape.142
  3.6 0.0 copy-done
  3.6 9.7 %gather_fusion = bf16[2048,1024]{1,0:T(8,128)(2,1)} fusion(bf16[1024,1024]{1,0:T(8,128)(2,1)S(1)} %copy-done, s32[2048]{0:T(1024)S(1)} %broadcast_clamp_fusion), kind=kCustom, calls=%fused_computation | custom fusion | bytes 8396800 | tf_op jit(solution)/shard_map/jit(_take)/gather | solution.py:42
  13.3 11.6 %gather.7 = bf16[128,256,64]{2,1,0:T(8,128)(2,1)} reshape(bf16[2048,1024]{1,0:T(8,128)(2,1)} %gather_fusion) | data formatting | bytes 8388608 | tf_op jit(solution)/shard_map/jit(_take)/gather | solution.py:42
  24.8 0.1 copy.36
  25.0 0.0 copy-start.1
  25.0 9.8 %fusion = f32[128,64,16]{1,2,0:T(8,128)} fusion(bf16[128,16,256]{2,1,0:T(8,128)(2,1)} %param.7, bf16[128,256,64]{2,1,0:T(8,128)(2,1)} %gather.7, pred[128,256]{1,0:T(8,128)(4,1)S(1)} %copy.36), kind=kOutput, calls=%fused_computation.13 | convolution fusion | flops 69206016 | bytes 5799936 | tf_op jit(solution)/shard_map/jnc,jtn->jct/dot_general | solution.py:44
  34.8 1.7 %copy.39 = f32[128,64,16]{0,2,1:T(8,128)S(1)} copy(f32[128,64,16]{1,2,0:T(8,128)} %fusion) | data formatting | bytes 1048576 | tf_op jit(solution)/shard_map/jnc,jtn->jct/dot_general | solution.py:44
  36.5 0.2 copy.40
  36.7 0.1 add_reduce_fusion.2
  36.9 0.1 add_reduce_fusion
  37.0 1.1 scatter_custom_fusion.1
  38.1 0.7 collective-permute-start.1
  38.8 0.0 copy-done.1
  38.8 1.0 scatter_custom_fusion
  39.8 0.0 collective-permute-start
  39.8 1.7 %scatter_custom_fusion.4 = f32[64,1024]{1,0:T(8,128)} fusion(s32[128]{0:T(128)S(1)} %get-tuple-element.8, f32[128,1024]{1,0:T(8,128)S(1)} %copy.40, f32[]{:T(128)} %constant.97.clone.1), kind=kCustom, calls=%fused_computation.23 | custom fusion | bytes 262148 | tf_op jit(solution)/shard_map/scatter | solution.py:59
  41.4 3.9 %collective-permute-start.3 = (f32[64,1024]{1,0:T(8,128)}, f32[64,1024]{1,0:T(8,128)S(1)}, u32[]{:S(2)}, u32[]{:S(2)}) collective-permute-start(f32[64,1024]{1,0:T(8,128)} %scatter_custom_fusion.4), channel_id=1, source_target_pairs={{1008,0},{0,16},{16,32},{32,48},{48,64},{64,80},{80,96},{96,112},{... | collective-permute-start | bytes 786440 | tf_op jit(solution)/shard_map/ppermute | solution.py:13
  45.4 1.0 scatter_custom_fusion.3
  46.4 3.1 %collective-permute-start.2 = (f32[64]{0:T(128)S(1)}, f32[64]{0:T(128)S(1)}, u32[]{:S(2)}, u32[]{:S(2)}) collective-permute-start(f32[64]{0:T(128)S(1)} %scatter_custom_fusion.3), channel_id=1, source_target_pairs={{1008,0},{0,16},{16,32},{32,48},{48,64},{64,80},{80,96},{96,112},{... | collective-permute-start | bytes 776 | tf_op jit(solution)/shard_map/ppermute | solution.py:13
  49.5 1.7 %scatter_custom_fusion.7 = f32[64,1024]{1,0:T(8,128)} fusion(s32[128]{0:T(128)S(1)} %get-tuple-element.9, f32[128,1024]{1,0:T(8,128)S(1)} %copy.40, f32[]{:T(128)} %constant.97.clone.1), kind=kCustom, calls=%fused_computation.21 | custom fusion | bytes 262148 | tf_op jit(solution)/shard_map/scatter | solution.py:59
  51.2 5.2 %collective-permute-start.5 = (f32[64,1024]{1,0:T(8,128)}, f32[64,1024]{1,0:T(8,128)}, u32[]{:S(2)}, u32[]{:S(2)}) collective-permute-start(f32[64,1024]{1,0:T(8,128)} %scatter_custom_fusion.7), channel_id=1, source_target_pairs={{992,0},{1008,16},{0,32},{16,48},{32,64},{48,80},{64,96},{80,112},... | collective-permute-start | bytes 786440 | tf_op jit(solution)/shard_map/ppermute | solution.py:13
  56.4 1.0 scatter_custom_fusion.6
  57.4 1.7 %scatter_custom_fusion.10 = f32[64,1024]{1,0:T(8,128)} fusion(s32[128]{0:T(128)S(1)} %get-tuple-element.7, f32[128,1024]{1,0:T(8,128)S(1)} %copy.40, f32[]{:T(128)} %constant.97.clone.1), kind=kCustom, calls=%fused_computation.19 | custom fusion | bytes 262148 | tf_op jit(solution)/shard_map/scatter | solution.py:59
  59.1 1.0 scatter_custom_fusion.9
  60.1 0.0 collective-permute-done
  60.1 2.2 %collective-permute-start.4 = (f32[64]{0:T(128)S(1)}, f32[64]{0:T(128)S(1)}, u32[]{:S(2)}, u32[]{:S(2)}) collective-permute-start(f32[64]{0:T(128)S(1)} %scatter_custom_fusion.6), channel_id=1, source_target_pairs={{992,0},{1008,16},{0,32},{16,48},{32,64},{48,80},{64,96},{80,112},... | collective-permute-start | bytes 776 | tf_op jit(solution)/shard_map/ppermute | solution.py:13
  62.4 0.0 collective-permute-done.2
  62.4 4.1 %collective-permute-start.7 = (f32[64,1024]{1,0:T(8,128)}, f32[64,1024]{1,0:T(8,128)}, u32[]{:S(2)}, u32[]{:S(2)}) collective-permute-start(f32[64,1024]{1,0:T(8,128)} %scatter_custom_fusion.10), channel_id=1, source_target_pairs={{976,0},{992,16},{1008,32},{0,48},{16,64},{32,80},{48,96},{64,112}... | collective-permute-start | bytes 786440 | tf_op jit(solution)/shard_map/ppermute | solution.py:13
  66.5 2.1 %collective-permute-done.4 = f32[64]{0:T(128)S(1)} collective-permute-done((f32[64]{0:T(128)S(1)}, f32[64]{0:T(128)S(1)}, u32[]{:S(2)}, u32[]{:S(2)}) %collective-permute-start.4) | collective-permute-done | bytes 288 | tf_op jit(solution)/shard_map/ppermute | solution.py:13
  68.6 4.0 %collective-permute-start.6 = (f32[64]{0:T(128)S(1)}, f32[64]{0:T(128)S(1)}, u32[]{:S(2)}, u32[]{:S(2)}) collective-permute-start(f32[64]{0:T(128)S(1)} %scatter_custom_fusion.9), channel_id=1, source_target_pairs={{976,0},{992,16},{1008,32},{0,48},{16,64},{32,80},{48,96},{64,112}... | collective-permute-start | bytes 776 | tf_op jit(solution)/shard_map/ppermute | solution.py:13
  72.7 11.9 %collective-permute-done.6 = f32[64]{0:T(128)S(1)} collective-permute-done((f32[64]{0:T(128)S(1)}, f32[64]{0:T(128)S(1)}, u32[]{:S(2)}, u32[]{:S(2)}) %collective-permute-start.6) | collective-permute-done | bytes 288 | tf_op jit(solution)/shard_map/ppermute | solution.py:13
  84.6 0.0 collective-permute-done.1
  84.6 1.8 %scatter_custom_fusion.2 = f32[256,1024]{1,0:T(8,128)S(1)} fusion(s32[64]{0:T(128)S(1)} %compare_select_fusion.7, f32[64,1024]{1,0:T(8,128)} %collective-permute-done.1, f32[]{:T(128)} %constant.97.clone.1), kind=kCustom, calls=%fused_computation.17 | custom fusion | flops 65536 | bytes 1049088 | tf_op jit(solution)/shard_map/scatter-add | solution.py:30
  86.4 0.0 collective-permute-done.3
  86.4 1.5 %scatter_fusion = f32[256,1024]{1,0:T(8,128)S(1)} fusion(f32[256,1024]{1,0:T(8,128)S(1)} %scatter_custom_fusion.2, s32[64]{0:T(128)S(1)} %compare_select_fusion.5, f32[64,1024]{1,0:T(8,128)S(1)} %collective-permute-done.3), kind=kCustom, calls=%fused_computation.6 | custom fusion | flops 65536 | bytes 786688 | tf_op jit(solution)/shard_map/scatter-add | solution.py:30
  87.9 0.0 collective-permute-done.5
  87.9 1.9 %scatter_fusion.1 = f32[256,1024]{1,0:T(8,128)S(1)} fusion(f32[256,1024]{1,0:T(8,128)S(1)} %scatter_fusion, s32[64]{0:T(128)S(1)} %compare_select_fusion.3, f32[64,1024]{1,0:T(8,128)} %collective-permute-done.5), kind=kCustom, calls=%fused_computation.9 | custom fusion | flops 65536 | bytes 786688 | tf_op jit(solution)/shard_map/scatter-add | solution.py:30
  89.9 0.0 collective-permute-done.7
  89.9 1.9 %scatter_fusion.2 = f32[256,1024]{1,0:T(8,128)S(1)} fusion(f32[256,1024]{1,0:T(8,128)S(1)} %scatter_fusion.1, s32[64]{0:T(128)S(1)} %compare_select_fusion.1, f32[64,1024]{1,0:T(8,128)} %collective-permute-done.7), kind=kCustom, calls=%fused_computation.12 | custom fusion | flops 65536 | bytes 786688 | tf_op jit(solution)/shard_map/scatter-add | solution.py:30
  91.8 48.8 %all_to_all.5 = f32[16,16,1024]{2,1,0:T(8,128)} all-to-all(f32[16,16,1024]{2,1,0:T(8,128)S(1)} %bitcast.18), channel_id=1, replica_groups=mesh['curve'=64,'lev'=16] {'lev'}, dimensions={0} | all-to-all | bytes 2097152 | tf_op jit(solution)/shard_map/all_to_all | solution.py:23
  140.6 1.3 reduce_sum.9
  141.9 0.2 reshape.134
  142.1 0.2 copy.47
  142.3 0.7 copy.48
  (9 shorter events, 0.1 us)
Async XLA Ops:
  0.0 3.6 %copy-start = (bf16[1024,1024]{1,0:T(8,128)(2,1)S(1)}, bf16[1024,1024]{1,0:T(8,128)(2,1)}, u32[]{:S(2)}) copy-start(bf16[1024,1024]{1,0:T(8,128)(2,1)} %param.4) | copy-start | bytes 6291460
  25.0 13.8 %copy-start.1 = (s32[128]{0:T(128)S(1)}, s32[128]{0:T(128)}, u32[]{:S(2)}) copy-start(s32[128]{0:T(128)} %param.6) | copy-start | bytes 1540
  38.1 46.5 %collective-permute-start.1 = (f32[64,1024]{1,0:T(8,128)S(1)}, f32[64,1024]{1,0:T(8,128)}, u32[]{:S(2)}, u32[]{:S(2)}) collective-permute-start(f32[64,1024]{1,0:T(8,128)S(1)} %scatter_custom_fusion.1), channel_id=1, source_target_pairs={{0,0},{16,16},{32,32},{48,48},{64,64},{80,80},{96,96},{112,112},{1... | collective-permute-start | bytes 786440 | tf_op jit(solution)/shard_map/ppermute | solution.py:13
  39.8 20.3 %collective-permute-start = (f32[64]{0:T(128)S(1)}, f32[64]{0:T(128)S(1)}, u32[]{:S(2)}, u32[]{:S(2)}) collective-permute-start(f32[64]{0:T(128)S(1)} %scatter_custom_fusion), channel_id=1, source_target_pairs={{0,0},{16,16},{32,32},{48,48},{64,64},{80,80},{96,96},{112,112},{1... | collective-permute-start | bytes 776 | tf_op jit(solution)/shard_map/ppermute | solution.py:13
  41.4 45.0 %collective-permute-start.3 = (f32[64,1024]{1,0:T(8,128)}, f32[64,1024]{1,0:T(8,128)S(1)}, u32[]{:S(2)}, u32[]{:S(2)}) collective-permute-start(f32[64,1024]{1,0:T(8,128)} %scatter_custom_fusion.4), channel_id=1, source_target_pairs={{1008,0},{0,16},{16,32},{32,48},{48,64},{64,80},{80,96},{96,112},{... | collective-permute-start | bytes 786440 | tf_op jit(solution)/shard_map/ppermute | solution.py:13
  46.4 16.0 %collective-permute-start.2 = (f32[64]{0:T(128)S(1)}, f32[64]{0:T(128)S(1)}, u32[]{:S(2)}, u32[]{:S(2)}) collective-permute-start(f32[64]{0:T(128)S(1)} %scatter_custom_fusion.3), channel_id=1, source_target_pairs={{1008,0},{0,16},{16,32},{32,48},{48,64},{64,80},{80,96},{96,112},{... | collective-permute-start | bytes 776 | tf_op jit(solution)/shard_map/ppermute | solution.py:13
  51.2 36.8 %collective-permute-start.5 = (f32[64,1024]{1,0:T(8,128)}, f32[64,1024]{1,0:T(8,128)}, u32[]{:S(2)}, u32[]{:S(2)}) collective-permute-start(f32[64,1024]{1,0:T(8,128)} %scatter_custom_fusion.7), channel_id=1, source_target_pairs={{992,0},{1008,16},{0,32},{16,48},{32,64},{48,80},{64,96},{80,112},... | collective-permute-start | bytes 786440 | tf_op jit(solution)/shard_map/ppermute | solution.py:13
  60.1 8.5 %collective-permute-start.4 = (f32[64]{0:T(128)S(1)}, f32[64]{0:T(128)S(1)}, u32[]{:S(2)}, u32[]{:S(2)}) collective-permute-start(f32[64]{0:T(128)S(1)} %scatter_custom_fusion.6), channel_id=1, source_target_pairs={{992,0},{1008,16},{0,32},{16,48},{32,64},{48,80},{64,96},{80,112},... | collective-permute-start | bytes 776 | tf_op jit(solution)/shard_map/ppermute | solution.py:13
  62.4 27.5 %collective-permute-start.7 = (f32[64,1024]{1,0:T(8,128)}, f32[64,1024]{1,0:T(8,128)}, u32[]{:S(2)}, u32[]{:S(2)}) collective-permute-start(f32[64,1024]{1,0:T(8,128)} %scatter_custom_fusion.10), channel_id=1, source_target_pairs={{976,0},{992,16},{1008,32},{0,48},{16,64},{32,80},{48,96},{64,112}... | collective-permute-start | bytes 786440 | tf_op jit(solution)/shard_map/ppermute | solution.py:13
  68.6 16.0 %collective-permute-start.6 = (f32[64]{0:T(128)S(1)}, f32[64]{0:T(128)S(1)}, u32[]{:S(2)}, u32[]{:S(2)}) collective-permute-start(f32[64]{0:T(128)S(1)} %scatter_custom_fusion.9), channel_id=1, source_target_pairs={{976,0},{992,16},{1008,32},{0,48},{16,64},{32,80},{48,96},{64,112}... | collective-permute-start | bytes 776 | tf_op jit(solution)/shard_map/ppermute | solution.py:13
where the time goes:
time: 144 us; the launch traced here: 143 us
  blocking collectives  48.8 us (34%)
  local copies, waits for them, and re-layouts  35.1 us (24%)
  starting transfers between devices  23.4 us (16%)
  waiting for transfers between devices  14.1 us (10%)
  other arithmetic  11.6 us (8%)
  matrix products  9.82 us (7%)
    all_to_all x1, blocking collectives, summed_on_arrival(): lax.all_to_all(pieces, axis, split_axis=0, concat_axis=0, tiled=True)  48.8 us
    ppermute x8, starting transfers between devices, shifted(): return lax.ppermute(block, axis, route)  23.4 us
    gather x2, local copies, waits for them, and re-layouts, per_device(): gathered = jnp.take(source_field, jnp.transpose(slot_elems), axis=0)  21.3 us
    ppermute x8, waiting for transfers between devices, shifted(): return lax.ppermute(block, axis, route)  14.1 us
    dot_general x1, matrix products, per_device(): jnp.einsum('jnc,jtn->jct', values, weights, preferred_element_type=jnp.fl...  9.82 us
    scatter-add x4, other arithmetic, deposit(): return band_total.at[dest_row].add(received, mode='drop')  7.13 us
    scatter x4, local copies, waits for them, and re-layouts, per_device(): sending = jnp.zeros((capacity, row_width), jnp.float32).at[position].set(...  6.12 us
    scatter x4, local copies, waits for them, and re-layouts, per_device(): jnp.full((capacity,), -1.0, jnp.float32).at[position]  3.9 us
  transfers between devices with their start and end apart: 8, of which 2 were waited for; matrix products, arithmetic and copies ran while one was open for 10% of the time, Pallas kernels for 0%

commit v1 on v0

v1 whole, which is shorter than its diff:
```python
import jax
import jax.numpy as jnp
from jax import lax
from jax.experimental import pallas as pl
from jax.experimental.pallas import tpu as pltpu
from jax.sharding import PartitionSpec as P

NB = 4
LANES = 128
RESIDUES = 64
CLASSES = 4
PEERS = 16
CHUNK = 65
PIECES = 4
UNROLL = 32


def partials_kernel(
    elems, tiles, source, weights, out, nodes, regrouped, named, bf_source, bf_weights, row_of, sems
):
    band_index = lax.axis_index("curve")
    weights_in = pltpu.make_async_copy(weights, bf_weights, sems.at[PIECES])
    weights_in.start()
    rows_each = 1024 // PIECES
    source_in = []
    for k in range(PIECES):
        part = pl.ds(k * rows_each, rows_each)
        source_in.append(pltpu.make_async_copy(source.at[part], bf_source.at[part], sems.at[k]))
        source_in[k].start()

    for residue in range(RESIDUES):
        peer = ((residue >> 2) & 3) * CLASSES + (residue >> 4)
        row_of[residue] = peer * CHUNK + (residue & 3) * 16

    old = lax.broadcasted_iota(jnp.int32, (256, 256), 0)
    new = lax.broadcasted_iota(jnp.int32, (256, 256), 1)
    wanted = ((new >> 3) & 15) * 16 + (new & 7) * 2 + (new >> 7)
    reorder = jnp.where(old == wanted, 1.0, 0.0).astype(jnp.bfloat16)
    weights_in.wait()

    def regroup(i, carry):
        at = pl.ds(i * 32, 32)
        moved = jnp.dot(bf_weights[at].reshape(512, 256), reorder, preferred_element_type=jnp.float32)
        moved = moved.astype(jnp.bfloat16)
        regrouped[at, 0] = moved[:, :LANES].reshape(32, 16, LANES)
        regrouped[at, 1] = moved[:, LANES:].reshape(32, 16, LANES)
        return carry

    lax.fori_loop(0, 4, regroup, 0)

    def unfold(i, carry):
        for half in range(2):
            at = i * 2 + half
            block = bf_source[pl.ds(pl.multiple_of(at * 16, 16), 16), :].astype(jnp.float32)
            for pair in range(8):
                nodes[pl.ds(at * 128 + pair, 16, stride=8), :] = block[
                    :, pair * LANES : (pair + 1) * LANES
                ]
        return carry

    for k in range(PIECES):
        source_in[k].wait()
        lax.fori_loop(k * rows_each // 32, (k + 1) * rows_each // 32, unfold, 0)

    low_half = lax.broadcasted_iota(jnp.int32, (8, LANES), 1) < 64

    def one_slot(s):
        rows = [
            nodes[pl.ds(pl.multiple_of(elems[e * 128 + s] * 8, 8), 8), :] for e in range(16)
        ]
        values = jnp.concatenate(rows, axis=0).astype(jnp.bfloat16)
        product = jnp.dot(
            regrouped[s].reshape(32, LANES), values, preferred_element_type=jnp.float32
        )
        first, second, third, fourth = (product[8 * k : 8 * k + 8] for k in range(4))
        straight = jnp.where(low_half, first, fourth)
        crossed = jnp.where(low_half, second, third)
        partial = straight + pltpu.roll(crossed, 64, 1)
        tile = tiles[s]
        residue = tile & 63
        row = row_of[residue]
        row_of[residue] = row + 8
        out[pl.ds(row, 8), :] = partial
        named[pl.ds(row >> 3, 1), :] = jnp.full((1, LANES), tile, jnp.int32)

    def slots(i, carry):
        for k in range(UNROLL):
            one_slot(i * UNROLL + k)
        return carry

    lax.fori_loop(0, 128 // UNROLL, slots, 0)

    diagonal = lax.broadcasted_iota(jnp.int32, (8, LANES), 0) == lax.broadcasted_iota(
        jnp.int32, (8, LANES), 1
    )
    for peer in range(PEERS):
        tags = (named[pl.ds(peer * 8 + (peer >> 3), 8), :] - band_index * 256) & 1023
        tags = ((tags >> 6) << 2) | (tags & 3)
        tags = jnp.where(diagonal, tags.astype(jnp.float32), 0.0)
        out[pl.ds(peer * CHUNK + 64, 1), :] = jnp.sum(tags, axis=0, keepdims=True)


def bins_kernel(arrived, *outs):
    diagonal = lax.broadcasted_iota(jnp.int32, (8, LANES), 0) == lax.broadcasted_iota(
        jnp.int32, (8, LANES), 1
    )
    bin_ids = lax.broadcasted_iota(jnp.int32, (8, LANES), 1).astype(jnp.float32)
    chosen = []
    for peer in range(PEERS):
        tags = jnp.where(diagonal, arrived[pl.ds(peer * CHUNK + 64, 8, stride=0), :], 0.0)
        chosen.append(jnp.where(jnp.sum(tags, axis=1, keepdims=True) == bin_ids, 1.0, 0.0))
    chosen = jnp.transpose(jnp.concatenate(chosen, axis=0))[:64].astype(jnp.bfloat16)
    for i in range(8):
        exact = jnp.concatenate(
            [arrived[pl.ds(peer * CHUNK + i, 8, stride=8), :] for peer in range(PEERS)], axis=0
        )
        high = exact.astype(jnp.bfloat16)
        rest = exact - high.astype(jnp.float32)
        middle = rest.astype(jnp.bfloat16)
        low = (rest - middle.astype(jnp.float32)).astype(jnp.bfloat16)
        total = sum(
            jnp.dot(chosen, part, preferred_element_type=jnp.float32) for part in (low, middle, high)
        )
        for step in range(NB):
            outs[step][pl.ds(i, 16, stride=8), :] = total[16 * step : 16 * step + 16]


def boxes_kernel(tiles, out):
    for half in range(2):
        rows = []
        for k in range(8):
            tile = tiles[pl.ds((half * 8 + k) * 8, 8), :]
            rows += [tile, pltpu.roll(tile, 64, 1)]
        turned = jnp.transpose(jnp.concatenate(rows, axis=0))
        out[:, half * LANES : (half + 1) * LANES] = turned[:64]


def in_vmem():
    return pl.BlockSpec(memory_space=pltpu.VMEM)


def budget(mib):
    return pltpu.CompilerParams(vmem_limit_bytes=mib * 2**20)


def partials(slot_elems, slot_tiles, source_field, weights):
    scalars = pl.BlockSpec(memory_space=pltpu.SMEM)
    outside = pl.BlockSpec(memory_space=pltpu.HBM)
    return pl.pallas_call(
        partials_kernel,
        out_shape=jax.ShapeDtypeStruct((PEERS * CHUNK, LANES), jnp.float32),
        in_specs=[scalars, scalars, outside, outside],
        out_specs=in_vmem(),
        scratch_shapes=[
            pltpu.VMEM((8192, LANES), jnp.float32),
            pltpu.VMEM((128, 2, 16, LANES), jnp.bfloat16),
            pltpu.VMEM((136, LANES), jnp.int32),
            pltpu.VMEM((1024, 1024), jnp.bfloat16),
            pltpu.VMEM((128, 16, 256), jnp.bfloat16),
            pltpu.SMEM((RESIDUES,), jnp.int32),
            pltpu.SemaphoreType.DMA((PIECES + 1,)),
        ],
        compiler_params=budget(53),
        name="partials",
    )(slot_elems.reshape(-1), slot_tiles, source_field, weights)


def bins(arrived):
    return pl.pallas_call(
        bins_kernel,
        out_shape=[jax.ShapeDtypeStruct((LANES, LANES), jnp.float32)] * NB,
        in_specs=[in_vmem()],
        out_specs=[in_vmem()] * NB,
        compiler_params=budget(8),
        name="bins",
    )(arrived)


def boxes(tiles):
    return pl.pallas_call(
        boxes_kernel,
        out_shape=jax.ShapeDtypeStruct((64, 256), jnp.float32),
        in_specs=[in_vmem()],
        out_specs=in_vmem(),
        compiler_params=budget(4),
        name="boxes",
    )(tiles)


def per_device(source_field, slot_elems, slot_tiles, weights):
    curve_size = lax.axis_size("curve")
    lev_size = lax.axis_size("lev")
    sending = partials(slot_elems, slot_tiles, source_field, weights)
    arrived = lax.all_to_all(
        sending.reshape(lev_size, 1, CHUNK * LANES), "lev", split_axis=0, concat_axis=0, tiled=True
    )
    steps = bins(arrived.reshape(PEERS * CHUNK, LANES))
    total = steps[0]
    for step in range(NB - 1, 0, -1):
        route = [(i, (i + step) % curve_size) for i in range(curve_size)]
        total = total + lax.ppermute(steps[step], "curve", route)
    groups = [[c + CLASSES * k for k in range(lev_size // CLASSES)] for c in range(CLASSES)]
    mine = lax.all_to_all(
        total.reshape(4, 32, LANES),
        "lev",
        split_axis=0,
        concat_axis=0,
        tiled=True,
        axis_index_groups=groups,
    )
    return boxes(mine.reshape(LANES, LANES))


def solution(mesh):
    placed = (
        P(("curve", "lev"), None),
        P(None, ("curve", "lev")),
        P(("curve", "lev")),
        P(("curve", "lev"), None, None),
    )
    return jax.shard_map(
        per_device, mesh=mesh, in_specs=placed, out_specs=P(None, ("curve", "lev")), check_vma=False
    )
```

time: 144 us -> 74.7 us (0.52)
  the two profiles are of different devices: /device:TPU:1 before, /device:TPU:64 now
where the time goes in v1:
time: 74.7 us; the launch traced here: 74.4 us
  blocking collectives  45.5 us (61%)
  starting transfers between devices  12.4 us (17%)
  Pallas kernels  8.14 us (11%)
  waiting for transfers between devices  6.97 us (9%)
  local copies, waits for them, and re-layouts  1.35 us (2%)
    all_to_all x1, blocking collectives, per_device(): lax.all_to_all(sending.reshape(lev_size, 1, CHUNK * LANES), 'lev', split_...  34.9 us
    ppermute x3, starting transfers between devices, per_device(): total = total + lax.ppermute(steps[step], 'curve', route)  12.4 us
    all_to_all x1, blocking collectives, per_device(): lax.all_to_all(total.reshape(4, 32, LANES), 'lev', split_axis=0, concat_a...  10.6 us
    ppermute x3, waiting for transfers between devices, per_device(): total = total + lax.ppermute(steps[step], 'curve', route)  6.97 us
    pallas_call x1, Pallas kernels, partials(): pl.pallas_call(partials_kernel, out_shape=jax.ShapeDtypeStruct((PEERS * C...  6.89 us
  transfers between devices with their start and end apart: 3, of which 3 were waited for; matrix products, arithmetic and copies ran while one was open for 0% of the time, Pallas kernels for 0%

profile of v1, /device:TPU:64, one launch (start us, length us, event | category | flops | bytes accessed | tf_op | source)
XLA Modules:
  0.0 74.4 jit_solution(6052329945774570317)
XLA Ops:
  0.0 0.0 copy-start
  0.0 0.7 copy-done
  0.7 0.0 copy-start.1
  0.7 0.7 copy-done.1
  1.4 6.9 %partials.1 = f32[1040,128]{1,0:T(8,128)S(1)} custom-call(s32[2048]{0:T(1024)S(1)} %bitcast.8, s32[128]{0:T(128)S(1)} %copy-done.1, bf16[1024,1024]{1,0:T(8,128)(2,1)} %source.1, bf16[128,16,256]{2,1,0:T(8,128)(2,1)} %weights.1), custom_call_target="tpu_custom_call" | custom-call | tf_op jit(solution)/shard_map/partials/pallas_call | solution.py:149
  8.2 34.9 %all_to_all.10 = f32[16,1,8320]{2,1,0:T(1,128)S(1)} all-to-all(f32[16,1,8320]{2,1,0:T(1,128)S(1)} %bitcast.6), channel_id=1, replica_groups=mesh['curve'=64,'lev'=16] {'lev'}, dimensions={0} | all-to-all | bytes 1064960 | tf_op jit(solution)/shard_map/all_to_all | solution.py:194
  43.2 0.5 bins.1
  43.7 5.3 %collective-permute-start = (f32[128,128]{1,0:T(8,128)S(1)}, f32[128,128]{1,0:T(8,128)S(1)}, u32[]{:S(2)}, u32[]{:S(2)}) collective-permute-start(f32[128,128]{1,0:T(8,128)S(1)} %get-tuple-element.10), channel_id=1, source_target_pairs={{0,48},{16,64},{32,80},{48,96},{64,112},{80,128},{96,144},{112,160... | collective-permute-start | bytes 196616 | tf_op jit(solution)/shard_map/ppermute | solution.py:201
  48.9 4.6 %collective-permute-start.1 = (f32[128,128]{1,0:T(8,128)S(1)}, f32[128,128]{1,0:T(8,128)S(1)}, u32[]{:S(2)}, u32[]{:S(2)}) collective-permute-start(f32[128,128]{1,0:T(8,128)S(1)} %get-tuple-element.11), channel_id=1, source_target_pairs={{0,32},{16,48},{32,64},{48,80},{64,96},{80,112},{96,128},{112,144}... | collective-permute-start | bytes 196616 | tf_op jit(solution)/shard_map/ppermute | solution.py:201
  53.6 2.5 %collective-permute-start.2 = (f32[128,128]{1,0:T(8,128)S(1)}, f32[128,128]{1,0:T(8,128)S(1)}, u32[]{:S(2)}, u32[]{:S(2)}) collective-permute-start(f32[128,128]{1,0:T(8,128)S(1)} %get-tuple-element.12), channel_id=1, source_target_pairs={{0,16},{16,32},{32,48},{48,64},{64,80},{80,96},{96,112},{112,128},... | collective-permute-start | bytes 196616 | tf_op jit(solution)/shard_map/ppermute | solution.py:201
  56.1 0.4 collective-permute-done
  56.5 3.5 %collective-permute-done.1 = f32[128,128]{1,0:T(8,128)S(1)} collective-permute-done((f32[128,128]{1,0:T(8,128)S(1)}, f32[128,128]{1,0:T(8,128)S(1)}, u32[]{:S(2)}, u32[]{:S(2)}) %collective-permute-start.1) | collective-permute-done | bytes 65568 | tf_op jit(solution)/shard_map/ppermute | solution.py:201
  60.0 3.0 %collective-permute-done.2 = f32[128,128]{1,0:T(8,128)S(1)} collective-permute-done((f32[128,128]{1,0:T(8,128)S(1)}, f32[128,128]{1,0:T(8,128)S(1)}, u32[]{:S(2)}, u32[]{:S(2)}) %collective-permute-start.2) | collective-permute-done | bytes 65568 | tf_op jit(solution)/shard_map/ppermute | solution.py:201
  63.1 10.6 %all_to_all.11 = f32[4,32,128]{2,1,0:T(8,128)S(1)} all-to-all(f32[4,32,128]{2,1,0:T(8,128)S(1)} %bitcast.9), channel_id=1, replica_groups={{0,4,8,12},{1,5,9,13},{2,6,10,14},{3,7,11,15},{16,20,24,28},{17,21,25,2..., dimensions={0} | all-to-all | bytes 131072 | tf_op jit(solution)/shard_map/all_to_all | solution.py:203
  73.6 0.8 %boxes.1 = f32[64,256]{1,0:T(8,128)} custom-call(f32[128,128]{1,0:T(8,128)S(1)} %bitcast.7), custom_call_target="tpu_custom_call" | custom-call | tf_op jit(solution)/shard_map/boxes/pallas_call | solution.py:180
  (1 shorter events, 0.0 us)
Async XLA Ops:
  0.0 0.7 copy-start
  0.7 0.7 copy-start.1
  43.7 12.8 %collective-permute-start = (f32[128,128]{1,0:T(8,128)S(1)}, f32[128,128]{1,0:T(8,128)S(1)}, u32[]{:S(2)}, u32[]{:S(2)}) collective-permute-start(f32[128,128]{1,0:T(8,128)S(1)} %get-tuple-element.10), channel_id=1, source_target_pairs={{0,48},{16,64},{32,80},{48,96},{64,112},{80,128},{96,144},{112,160... | collective-permute-start | bytes 196616 | tf_op jit(solution)/shard_map/ppermute | solution.py:201
  48.9 11.1 %collective-permute-start.1 = (f32[128,128]{1,0:T(8,128)S(1)}, f32[128,128]{1,0:T(8,128)S(1)}, u32[]{:S(2)}, u32[]{:S(2)}) collective-permute-start(f32[128,128]{1,0:T(8,128)S(1)} %get-tuple-element.11), channel_id=1, source_target_pairs={{0,32},{16,48},{32,64},{48,80},{64,96},{80,112},{96,128},{112,144}... | collective-permute-start | bytes 196616 | tf_op jit(solution)/shard_map/ppermute | solution.py:201
  53.6 9.5 %collective-permute-start.2 = (f32[128,128]{1,0:T(8,128)S(1)}, f32[128,128]{1,0:T(8,128)S(1)}, u32[]{:S(2)}, u32[]{:S(2)}) collective-permute-start(f32[128,128]{1,0:T(8,128)S(1)} %get-tuple-element.12), channel_id=1, source_target_pairs={{0,16},{16,32},{32,48},{48,64},{64,80},{80,96},{96,112},{112,128},... | collective-permute-start | bytes 196616 | tf_op jit(solution)/shard_map/ppermute | solution.py:201

commit v2 on v1

--- a/solution.py
+++ b/solution.py
@@ -12,13 +12,32 @@
 PEERS = 16
 CHUNK = 65
 PIECES = 4
-UNROLL = 32
 
 
 def partials_kernel(
-    elems, tiles, source, weights, out, nodes, regrouped, named, bf_source, bf_weights, row_of, sems
+    slot_elems,
+    slot_tiles,
+    source,
+    weights,
+    out,
+    nodes,
+    regrouped,
+    named,
+    bf_source,
+    bf_weights,
+    elems,
+    elem_rows,
+    tiles,
+    row_of,
+    sems,
 ):
     band_index = lax.axis_index("curve")
+    scalars_in = [
+        pltpu.make_async_copy(slot_elems, elems, sems.at[PIECES + 1]),
+        pltpu.make_async_copy(slot_tiles, tiles, sems.at[PIECES + 2]),
+    ]
+    for copy in scalars_in:
+        copy.start()
     weights_in = pltpu.make_async_copy(weights, bf_weights, sems.at[PIECES])
     weights_in.start()
     rows_each = 1024 // PIECES
@@ -47,6 +66,11 @@
         return carry
 
     lax.fori_loop(0, 4, regroup, 0)
+
+    scalars_in[0].wait()
+    elems[...] = elems[...] * 8
+    scaled_in = pltpu.make_async_copy(elems, elem_rows, sems.at[PIECES + 3])
+    scaled_in.start()
 
     def unfold(i, carry):
         for half in range(2):
@@ -62,11 +86,13 @@
         source_in[k].wait()
         lax.fori_loop(k * rows_each // 32, (k + 1) * rows_each // 32, unfold, 0)
 
+    scaled_in.wait()
+    scalars_in[1].wait()
     low_half = lax.broadcasted_iota(jnp.int32, (8, LANES), 1) < 64
 
     def one_slot(s):
         rows = [
-            nodes[pl.ds(pl.multiple_of(elems[e * 128 + s] * 8, 8), 8), :] for e in range(16)
+            nodes[pl.ds(pl.multiple_of(elem_rows[e, s], 8), 8), :] for e in range(16)
         ]
         values = jnp.concatenate(rows, axis=0).astype(jnp.bfloat16)
         product = jnp.dot(
@@ -83,12 +109,8 @@
         out[pl.ds(row, 8), :] = partial
         named[pl.ds(row >> 3, 1), :] = jnp.full((1, LANES), tile, jnp.int32)
 
-    def slots(i, carry):
-        for k in range(UNROLL):
-            one_slot(i * UNROLL + k)
-        return carry
-
-    lax.fori_loop(0, 128 // UNROLL, slots, 0)
+    for s in range(128):
+        one_slot(s)
 
     diagonal = lax.broadcasted_iota(jnp.int32, (8, LANES), 0) == lax.broadcasted_iota(
         jnp.int32, (8, LANES), 1
@@ -122,7 +144,9 @@
             jnp.dot(chosen, part, preferred_element_type=jnp.float32) for part in (low, middle, high)
         )
         for step in range(NB):
-            outs[step][pl.ds(i, 16, stride=8), :] = total[16 * step : 16 * step + 16]
+            outs[step & 1][pl.ds((step >> 1) * LANES + i, 16, stride=8), :] = total[
+                16 * step : 16 * step + 16
+            ]
 
 
 def boxes_kernel(tiles, out):
@@ -144,12 +168,11 @@
 
 
 def partials(slot_elems, slot_tiles, source_field, weights):
-    scalars = pl.BlockSpec(memory_space=pltpu.SMEM)
     outside = pl.BlockSpec(memory_space=pltpu.HBM)
     return pl.pallas_call(
         partials_kernel,
         out_shape=jax.ShapeDtypeStruct((PEERS * CHUNK, LANES), jnp.float32),
-        in_specs=[scalars, scalars, outside, outside],
+        in_specs=[outside] * 4,
         out_specs=in_vmem(),
         scratch_shapes=[
             pltpu.VMEM((8192, LANES), jnp.float32),
@@ -157,20 +180,28 @@
             pltpu.VMEM((136, LANES), jnp.int32),
             pltpu.VMEM((1024, 1024), jnp.bfloat16),
             pltpu.VMEM((128, 16, 256), jnp.bfloat16),
+            pltpu.VMEM((16, 128), jnp.int32),
+            pltpu.SMEM((16, 128), jnp.int32),
+            pltpu.SMEM((128,), jnp.int32),
             pltpu.SMEM((RESIDUES,), jnp.int32),
-            pltpu.SemaphoreType.DMA((PIECES + 1,)),
+            pltpu.SemaphoreType.DMA((PIECES + 4,)),
         ],
         compiler_params=budget(53),
         name="partials",
-    )(slot_elems.reshape(-1), slot_tiles, source_field, weights)
+    )(
+        pltpu.with_memory_space_constraint(slot_elems, pltpu.HBM),
+        pltpu.with_memory_space_constraint(slot_tiles, pltpu.HBM),
+        source_field,
+        weights,
+    )
 
 
 def bins(arrived):
     return pl.pallas_call(
         bins_kernel,
-        out_shape=[jax.ShapeDtypeStruct((LANES, LANES), jnp.float32)] * NB,
+        out_shape=[jax.ShapeDtypeStruct((2 * LANES, LANES), jnp.float32)] * 2,
         in_specs=[in_vmem()],
-        out_specs=[in_vmem()] * NB,
+        out_specs=[in_vmem()] * 2,
         compiler_params=budget(8),
         name="bins",
     )(arrived)
@@ -187,18 +218,20 @@
     )(tiles)
 
 
+def ahead(block, distance):
+    size = lax.axis_size("curve")
+    return lax.ppermute(block, "curve", [(i, (i + distance) % size) for i in range(size)])
+
+
 def per_device(source_field, slot_elems, slot_tiles, weights):
-    curve_size = lax.axis_size("curve")
     lev_size = lax.axis_size("lev")
     sending = partials(slot_elems, slot_tiles, source_field, weights)
     arrived = lax.all_to_all(
         sending.reshape(lev_size, 1, CHUNK * LANES), "lev", split_axis=0, concat_axis=0, tiled=True
     )
-    steps = bins(arrived.reshape(PEERS * CHUNK, LANES))
-    total = steps[0]
-    for step in range(NB - 1, 0, -1):
-        route = [(i, (i + step) % curve_size) for i in range(curve_size)]
-        total = total + lax.ppermute(steps[step], "curve", route)
+    near, far = bins(arrived.reshape(PEERS * CHUNK, LANES))
+    far = ahead(far, 1)
+    total = near[:LANES] + far[:LANES] + ahead(near[LANES:] + far[LANES:], 2)
     groups = [[c + CLASSES * k for k in range(lev_size // CLASSES)] for c in range(CLASSES)]
     mine = lax.all_to_all(
         total.reshape(4, 32, LANES),

time: 74.7 us -> 72.6 us (0.972)
  waiting for transfers between devices: 6.97 us -> 15.5 us
  starting transfers between devices: 12.4 us -> 5.32 us
  Pallas kernels: 8.14 us -> 5.92 us
  local copies, waits for them, and re-layouts: 1.35 us -> 0 us
    ppermute x3 -> x2, waiting for transfers between devices: 6.97 us -> 15.5 us  [ahead(): lax.ppermute(block, 'curve', [(i, (i + distance) % size) for i in range(s...]
    ppermute x3 -> x2, starting transfers between devices: 12.4 us -> 5.32 us  [ahead(): lax.ppermute(block, 'curve', [(i, (i + distance) % size) for i in range(s...]
    pallas_call x1, Pallas kernels: 6.89 us -> 4.67 us  [partials(): pl.pallas_call(partials_kernel, out_shape=jax.ShapeDtypeStruct((PEERS * C...]
    unnamed x4 -> x0, local copies, waits for them, and re-layouts: 1.35 us -> none
  transfers between devices with their start and end apart: 3 -> 2, of which waited for: 3 -> 2; matrix products, arithmetic and copies ran while one was open for 0% -> 0% of each run, Pallas kernels for 0% -> 0%
where the time goes in v2:
time: 72.6 us; the launch traced here: 72.3 us
  blocking collectives  45.5 us (63%)
  waiting for transfers between devices  15.5 us (21%)
  Pallas kernels  5.92 us (8%)
  starting transfers between devices  5.32 us (7%)
    all_to_all x1, blocking collectives, per_device(): lax.all_to_all(sending.reshape(lev_size, 1, CHUNK * LANES), 'lev', split_...  34.9 us
    ppermute x2, waiting for transfers between devices, ahead(): lax.ppermute(block, 'curve', [(i, (i + distance) % size) for i in range(s...  15.5 us
    all_to_all x1, blocking collectives, per_device(): lax.all_to_all(total.reshape(4, 32, LANES), 'lev', split_axis=0, concat_a...  10.6 us
    ppermute x2, starting transfers between devices, ahead(): lax.ppermute(block, 'curve', [(i, (i + distance) % size) for i in range(s...  5.32 us
    pallas_call x1, Pallas kernels, partials(): pl.pallas_call(partials_kernel, out_shape=jax.ShapeDtypeStruct((PEERS * C...  4.67 us
  transfers between devices with their start and end apart: 2, of which 2 were waited for; matrix products, arithmetic and copies ran while one was open for 0% of the time, Pallas kernels for 0%

profile of v2, /device:TPU:64, one launch (start us, length us, event | category | flops | bytes accessed | tf_op | source)
XLA Modules:
  0.0 72.3 jit_solution(7984438012769762986)
XLA Ops:
  0.0 4.7 %partials.1 = f32[1040,128]{1,0:T(8,128)S(1)} custom-call(s32[16,128]{1,0:T(8,128)} %slot_elems.1, s32[128]{0:T(128)} %slot_tiles.1, bf16[1024,1024]{1,0:T(8,128)(2,1)} %source.1, bf16[128,16,256]{2,1,0:T(8,128)(2,1)} %weights.1), custom_call_target="tpu_custom_call" | custom-call | tf_op jit(solution)/shard_map/partials/pallas_call | solution.py:172
  4.7 34.9 %all_to_all.10 = f32[16,1,8320]{2,1,0:T(1,128)S(1)} all-to-all(f32[16,1,8320]{2,1,0:T(1,128)S(1)} %bitcast.5), channel_id=1, replica_groups=mesh['curve'=64,'lev'=16] {'lev'}, dimensions={0} | all-to-all | bytes 1064960 | tf_op jit(solution)/shard_map/all_to_all | solution.py:229
  39.6 0.5 bins.1
  40.1 3.4 %collective-permute-start = (f32[256,128]{1,0:T(8,128)S(1)}, f32[256,128]{1,0:T(8,128)S(1)}, u32[]{:S(2)}, u32[]{:S(2)}) collective-permute-start(f32[256,128]{1,0:T(8,128)S(1)} %get-tuple-element.8), channel_id=1, source_target_pairs={{0,16},{16,32},{32,48},{48,64},{64,80},{80,96},{96,112},{112,128},... | collective-permute-start | bytes 393224 | tf_op jit(solution)/shard_map/ppermute | solution.py:223
  43.5 7.1 %collective-permute-done = f32[256,128]{1,0:T(8,128)S(1)} collective-permute-done((f32[256,128]{1,0:T(8,128)S(1)}, f32[256,128]{1,0:T(8,128)S(1)}, u32[]{:S(2)}, u32[]{:S(2)}) %collective-permute-start) | collective-permute-done | bytes 131104 | tf_op jit(solution)/shard_map/ppermute | solution.py:223
  50.6 1.9 %collective-permute-start.1 = (f32[128,128]{1,0:T(8,128)S(1)}, f32[128,128]{1,0:T(8,128)S(1)}, u32[]{:S(2)}, u32[]{:S(2)}) collective-permute-start(f32[128,128]{1,0:T(8,128)S(1)} %slice_add_fusion), channel_id=1, source_target_pairs={{0,32},{16,48},{32,64},{48,80},{64,96},{80,112},{96,128},{112,144}... | collective-permute-start | bytes 196616 | tf_op jit(solution)/shard_map/ppermute | solution.py:223
  52.5 8.4 %collective-permute-done.1 = f32[128,128]{1,0:T(8,128)S(1)} collective-permute-done((f32[128,128]{1,0:T(8,128)S(1)}, f32[128,128]{1,0:T(8,128)S(1)}, u32[]{:S(2)}, u32[]{:S(2)}) %collective-permute-start.1) | collective-permute-done | bytes 65568 | tf_op jit(solution)/shard_map/ppermute | solution.py:223
  61.0 10.6 %all_to_all.11 = f32[4,32,128]{2,1,0:T(8,128)S(1)} all-to-all(f32[4,32,128]{2,1,0:T(8,128)S(1)} %bitcast.7), channel_id=1, replica_groups={{0,4,8,12},{1,5,9,13},{2,6,10,14},{3,7,11,15},{16,20,24,28},{17,21,25,2..., dimensions={0} | all-to-all | bytes 131072 | tf_op jit(solution)/shard_map/all_to_all | solution.py:236
  71.6 0.8 %boxes.1 = f32[64,256]{1,0:T(8,128)} custom-call(f32[128,128]{1,0:T(8,128)S(1)} %bitcast.6), custom_call_target="tpu_custom_call" | custom-call | tf_op jit(solution)/shard_map/boxes/pallas_call | solution.py:211
  (2 shorter events, 0.0 us)
Async XLA Ops:
  40.1 10.5 %collective-permute-start = (f32[256,128]{1,0:T(8,128)S(1)}, f32[256,128]{1,0:T(8,128)S(1)}, u32[]{:S(2)}, u32[]{:S(2)}) collective-permute-start(f32[256,128]{1,0:T(8,128)S(1)} %get-tuple-element.8), channel_id=1, source_target_pairs={{0,16},{16,32},{32,48},{48,64},{64,80},{80,96},{96,112},{112,128},... | collective-permute-start | bytes 393224 | tf_op jit(solution)/shard_map/ppermute | solution.py:223
  50.6 10.4 %collective-permute-start.1 = (f32[128,128]{1,0:T(8,128)S(1)}, f32[128,128]{1,0:T(8,128)S(1)}, u32[]{:S(2)}, u32[]{:S(2)}) collective-permute-start(f32[128,128]{1,0:T(8,128)S(1)} %slice_add_fusion), channel_id=1, source_target_pairs={{0,32},{16,48},{32,64},{48,80},{64,96},{80,112},{96,128},{112,144}... | collective-permute-start | bytes 196616 | tf_op jit(solution)/shard_map/ppermute | solution.py:223

commit v3 on v2

--- a/solution.py
+++ b/solution.py
@@ -5,12 +5,11 @@
 from jax.experimental.pallas import tpu as pltpu
 from jax.sharding import PartitionSpec as P
 
-NB = 4
 LANES = 128
 RESIDUES = 64
 CLASSES = 4
-PEERS = 16
-CHUNK = 65
+PEERS = 32
+CHUNK = 33
 PIECES = 4
 
 
@@ -48,8 +47,8 @@
         source_in[k].start()
 
     for residue in range(RESIDUES):
-        peer = ((residue >> 2) & 3) * CLASSES + (residue >> 4)
-        row_of[residue] = peer * CHUNK + (residue & 3) * 16
+        peer = ((residue >> 1) & 1) * 16 + ((residue >> 2) & 3) * CLASSES + (residue >> 4)
+        row_of[residue] = peer * CHUNK + (residue & 1) * 16
 
     old = lax.broadcasted_iota(jnp.int32, (256, 256), 0)
     new = lax.broadcasted_iota(jnp.int32, (256, 256), 1)
@@ -112,29 +111,29 @@
     for s in range(128):
         one_slot(s)
 
-    diagonal = lax.broadcasted_iota(jnp.int32, (8, LANES), 0) == lax.broadcasted_iota(
-        jnp.int32, (8, LANES), 1
+    diagonal = lax.broadcasted_iota(jnp.int32, (4, LANES), 0) == lax.broadcasted_iota(
+        jnp.int32, (4, LANES), 1
     )
     for peer in range(PEERS):
-        tags = (named[pl.ds(peer * 8 + (peer >> 3), 8), :] - band_index * 256) & 1023
-        tags = ((tags >> 6) << 2) | (tags & 3)
+        tags = named[pl.ds(peer * 4 + (peer >> 3), 4), :] - (band_index >> 1) * 512
+        tags = tags & 16383
+        tags = ((tags >> 6) << 1) | (tags & 1)
         tags = jnp.where(diagonal, tags.astype(jnp.float32), 0.0)
-        out[pl.ds(peer * CHUNK + 64, 1), :] = jnp.sum(tags, axis=0, keepdims=True)
-
-
-def bins_kernel(arrived, *outs):
-    diagonal = lax.broadcasted_iota(jnp.int32, (8, LANES), 0) == lax.broadcasted_iota(
-        jnp.int32, (8, LANES), 1
-    )
-    bin_ids = lax.broadcasted_iota(jnp.int32, (8, LANES), 1).astype(jnp.float32)
+        out[pl.ds(peer * CHUNK + 32, 1), :] = jnp.sum(tags, axis=0, keepdims=True)
+
+
+def bins_kernel(arrived, own, second, third):
+    lanes = lax.broadcasted_iota(jnp.int32, (PEERS, LANES), 1)
+    bin_ids = lanes.astype(jnp.float32)
+    named = arrived[pl.ds(32, PEERS, stride=CHUNK), :]
     chosen = []
-    for peer in range(PEERS):
-        tags = jnp.where(diagonal, arrived[pl.ds(peer * CHUNK + 64, 8, stride=0), :], 0.0)
-        chosen.append(jnp.where(jnp.sum(tags, axis=1, keepdims=True) == bin_ids, 1.0, 0.0))
-    chosen = jnp.transpose(jnp.concatenate(chosen, axis=0))[:64].astype(jnp.bfloat16)
+    for place in range(4):
+        tags = jnp.sum(jnp.where(lanes == place, named, 0.0), axis=1, keepdims=True)
+        chosen.append(jnp.where(tags == bin_ids, 1.0, 0.0))
+    chosen = jnp.transpose(jnp.concatenate(chosen, axis=0))[:40].astype(jnp.bfloat16)
     for i in range(8):
         exact = jnp.concatenate(
-            [arrived[pl.ds(peer * CHUNK + i, 8, stride=8), :] for peer in range(PEERS)], axis=0
+            [arrived[pl.ds(place * 8 + i, PEERS, stride=CHUNK), :] for place in range(4)], axis=0
         )
         high = exact.astype(jnp.bfloat16)
         rest = exact - high.astype(jnp.float32)
@@ -143,17 +142,17 @@
         total = sum(
             jnp.dot(chosen, part, preferred_element_type=jnp.float32) for part in (low, middle, high)
         )
-        for step in range(NB):
-            outs[step & 1][pl.ds((step >> 1) * LANES + i, 16, stride=8), :] = total[
-                16 * step : 16 * step + 16
-            ]
+        own[pl.ds(i, 16, stride=8), :] = total[:16]
+        second[pl.ds(i, 16, stride=8), :] = total[16:32]
+        third[pl.ds(i, 8, stride=8), :] = total[32:40]
 
 
 def boxes_kernel(tiles, out):
     for half in range(2):
         rows = []
-        for k in range(8):
-            tile = tiles[pl.ds((half * 8 + k) * 8, 8), :]
+        for k in range(half * 8, half * 8 + 8):
+            source = (((k >> 1) & 1) * 4 + (k >> 2)) * 2 + (k & 1)
+            tile = tiles[pl.ds(source * 8, 8), :]
             rows += [tile, pltpu.roll(tile, 64, 1)]
         turned = jnp.transpose(jnp.concatenate(rows, axis=0))
         out[:, half * LANES : (half + 1) * LANES] = turned[:64]
@@ -199,9 +198,9 @@
 def bins(arrived):
     return pl.pallas_call(
         bins_kernel,
-        out_shape=[jax.ShapeDtypeStruct((2 * LANES, LANES), jnp.float32)] * 2,
+        out_shape=[jax.ShapeDtypeStruct((rows, LANES), jnp.float32) for rows in (128, 128, 64)],
         in_specs=[in_vmem()],
-        out_specs=[in_vmem()] * 2,
+        out_specs=[in_vmem()] * 3,
         compiler_params=budget(8),
         name="bins",
     )(arrived)
@@ -223,24 +222,33 @@
     return lax.ppermute(block, "curve", [(i, (i + distance) % size) for i in range(size)])
 
 
-def per_device(source_field, slot_elems, slot_tiles, weights):
-    lev_size = lax.axis_size("lev")
-    sending = partials(slot_elems, slot_tiles, source_field, weights)
-    arrived = lax.all_to_all(
-        sending.reshape(lev_size, 1, CHUNK * LANES), "lev", split_axis=0, concat_axis=0, tiled=True
-    )
-    near, far = bins(arrived.reshape(PEERS * CHUNK, LANES))
-    far = ahead(far, 1)
-    total = near[:LANES] + far[:LANES] + ahead(near[LANES:] + far[LANES:], 2)
-    groups = [[c + CLASSES * k for k in range(lev_size // CLASSES)] for c in range(CLASSES)]
-    mine = lax.all_to_all(
-        total.reshape(4, 32, LANES),
-        "lev",
+def exchange(messages, groups):
+    return lax.all_to_all(
+        messages,
+        ("curve", "lev"),
         split_axis=0,
         concat_axis=0,
         tiled=True,
         axis_index_groups=groups,
     )
+
+
+def per_device(source_field, slot_elems, slot_tiles, weights):
+    lev_size = lax.axis_size("lev")
+    blocks = range(lax.axis_size("curve") // 2)
+    pairs = [[k * 2 * lev_size + m for m in range(2 * lev_size)] for k in blocks]
+    sending = partials(slot_elems, slot_tiles, source_field, weights)
+    arrived = exchange(sending.reshape(PEERS, 1, CHUNK * LANES), pairs)
+    own, second, third = bins(arrived.reshape(PEERS * CHUNK, LANES))
+    third = ahead(third, 4)
+    total = own + ahead(second, 2)
+    total = total + jnp.pad(third, ((0, 64), (0, 0)))
+    holders = [
+        [(2 * k + i) * lev_size + CLASSES * a + c for i in range(2) for a in range(4)]
+        for k in blocks
+        for c in range(CLASSES)
+    ]
+    mine = exchange(total.reshape(8, 16, LANES), holders)
     return boxes(mine.reshape(LANES, LANES))
 
 

time: 72.6 us -> 70.5 us (0.971)
  the two profiles are of different devices: /device:TPU:64 before, /device:TPU:4 now
where the time goes in v3:
time: 70.5 us; the launch traced here: 70.3 us
  blocking collectives  47.8 us (68%)
  starting transfers between devices  9.02 us (13%)
  waiting for transfers between devices  7.43 us (11%)
  Pallas kernels  5.96 us (8%)
    all_to_all x2, blocking collectives, exchange(): lax.all_to_all(messages, ('curve', 'lev'), split_axis=0, concat_axis=0, t...  47.8 us
    ppermute x2, starting transfers between devices, ahead(): lax.ppermute(block, 'curve', [(i, (i + distance) % size) for i in range(s...  9.02 us
    ppermute x2, waiting for transfers between devices, ahead(): lax.ppermute(block, 'curve', [(i, (i + distance) % size) for i in range(s...  7.43 us
    pallas_call x1, Pallas kernels, partials(): pl.pallas_call(partials_kernel, out_shape=jax.ShapeDtypeStruct((PEERS * C...  4.7 us
  transfers between devices with their start and end apart: 2, of which 1 were waited for; matrix products, arithmetic and copies ran while one was open for 0% of the time, Pallas kernels for 0%

profile of v3, /device:TPU:4, one launch (start us, length us, event | category | flops | bytes accessed | tf_op | source)
XLA Modules:
  0.0 70.3 jit_solution(17427884798462614778)
XLA Ops:
  0.0 4.7 %partials.1 = f32[1056,128]{1,0:T(8,128)S(1)} custom-call(s32[16,128]{1,0:T(8,128)} %slot_elems.1, s32[128]{0:T(128)} %slot_tiles.1, bf16[1024,1024]{1,0:T(8,128)(2,1)} %source.1, bf16[128,16,256]{2,1,0:T(8,128)(2,1)} %weights.1), custom_call_target="tpu_custom_call" | custom-call | tf_op jit(solution)/shard_map/partials/pallas_call | solution.py:171
  4.7 33.9 %all_to_all.10 = f32[32,1,4224]{2,1,0:T(1,128)S(1)} all-to-all(f32[32,1,4224]{2,1,0:T(1,128)S(1)} %bitcast.5), channel_id=1, replica_groups={{0,1,2,3,4,5,6,7,8,9,10,11,12,13,14,15,16,17,18,19,20,21,22,23,24,25,26..., dimensions={0} | all-to-all | bytes 1081344 | tf_op jit(solution)/shard_map/all_to_all | solution.py:226
  38.6 0.5 bins.1
  39.1 4.6 %collective-permute-start = (f32[128,128]{1,0:T(8,128)S(1)}, f32[128,128]{1,0:T(8,128)S(1)}, u32[]{:S(2)}, u32[]{:S(2)}) collective-permute-start(f32[128,128]{1,0:T(8,128)S(1)} %get-tuple-element.9), channel_id=1, source_target_pairs={{0,32},{16,48},{32,64},{48,80},{64,96},{80,112},{96,128},{112,144}... | collective-permute-start | bytes 196616 | tf_op jit(solution)/shard_map/ppermute | solution.py:222
  43.7 4.4 %collective-permute-start.1 = (f32[64,128]{1,0:T(8,128)S(1)}, f32[64,128]{1,0:T(8,128)S(1)}, u32[]{:S(2)}, u32[]{:S(2)}) collective-permute-start(f32[64,128]{1,0:T(8,128)S(1)} %get-tuple-element.10), channel_id=1, source_target_pairs={{0,64},{16,80},{32,96},{48,112},{64,128},{80,144},{96,160},{112,17... | collective-permute-start | bytes 98312 | tf_op jit(solution)/shard_map/ppermute | solution.py:222
  48.1 7.4 %collective-permute-done.1 = f32[64,128]{1,0:T(8,128)S(1)} collective-permute-done((f32[64,128]{1,0:T(8,128)S(1)}, f32[64,128]{1,0:T(8,128)S(1)}, u32[]{:S(2)}, u32[]{:S(2)}) %collective-permute-start.1) | collective-permute-done | bytes 32800 | tf_op jit(solution)/shard_map/ppermute | solution.py:222
  55.5 0.0 collective-permute-done
  55.6 14.0 %all_to_all.11 = f32[8,16,128]{2,1,0:T(8,128)S(1)} all-to-all(f32[8,16,128]{2,1,0:T(8,128)S(1)} %bitcast.7), channel_id=1, replica_groups={{0,4,8,12,16,20,24,28},{1,5,9,13,17,21,25,29},{2,6,10,14,18,22,26,30},{..., dimensions={0} | all-to-all | bytes 131072 | tf_op jit(solution)/shard_map/all_to_all | solution.py:226
  69.5 0.8 %boxes.1 = f32[64,256]{1,0:T(8,128)} custom-call(f32[128,128]{1,0:T(8,128)S(1)} %bitcast.6), custom_call_target="tpu_custom_call" | custom-call | tf_op jit(solution)/shard_map/boxes/pallas_call | solution.py:210
  (1 shorter events, 0.0 us)
Async XLA Ops:
  39.1 16.5 %collective-permute-start = (f32[128,128]{1,0:T(8,128)S(1)}, f32[128,128]{1,0:T(8,128)S(1)}, u32[]{:S(2)}, u32[]{:S(2)}) collective-permute-start(f32[128,128]{1,0:T(8,128)S(1)} %get-tuple-element.9), channel_id=1, source_target_pairs={{0,32},{16,48},{32,64},{48,80},{64,96},{80,112},{96,128},{112,144}... | collective-permute-start | bytes 196616 | tf_op jit(solution)/shard_map/ppermute | solution.py:222
  43.7 11.8 %collective-permute-start.1 = (f32[64,128]{1,0:T(8,128)S(1)}, f32[64,128]{1,0:T(8,128)S(1)}, u32[]{:S(2)}, u32[]{:S(2)}) collective-permute-start(f32[64,128]{1,0:T(8,128)S(1)} %get-tuple-element.10), channel_id=1, source_target_pairs={{0,64},{16,80},{32,96},{48,112},{64,128},{80,144},{96,160},{112,17... | collective-permute-start | bytes 98312 | tf_op jit(solution)/shard_map/ppermute | solution.py:222
